TPU v7x, 128 devices: a whole 4x4x4 slice. The times are simulated.
128 devices in a mesh: left: 32 (over z, y_lo, x), right: 4 (over y_hi, core).
Axes of the slice: x: 4, y: 4 (y_hi: 2, y_lo: 2; y = y_hi * 2 + y_lo), z: 4, core: 2. Of those that a mesh axis runs over, the one named last changes fastest.
Arguments:
- density: float32 [512, 512, 2048], P(None, 'left', 'right'), may hold values from -6 to 6
- symbol_x: float32 [512], replicated, may hold values from 0.3 to 3
- symbol_y: float32 [512], replicated, may hold values from 0.3 to 3
- symbol_z: float32 [2048], replicated, may hold values from 0.3 to 3
Outputs:
- spectrum: float32 [512, 512, 2048], P('left', 'right')
All inputs are finite; a program needn't handle non-finite values.
Results may differ from a plain program's by a relative error of at most 0.00007.
Values sent between devices are 32-bit elements; how exact they have to be, the bound alone decides.
No kernel may reach another device: no remote copies, remote signals or barrier semaphores. Data moves between devices by JAX's collectives and lax.ppermute only.
A program may use at most 192 MiB of HBM per device.

v0:
```python
import jax
import jax.numpy as jnp
from jax import lax
from jax.sharding import PartitionSpec as P


def split_up(x, dim, count):
    shape = x.shape
    parts = x.reshape(*shape[:dim], count, shape[dim] // count, *shape[dim + 1 :])
    return jnp.moveaxis(parts, dim, 0)


def edges_of(length, count):
    hop = length // count
    if hop >= 8:
        hop -= hop % 8
    return [hop * k for k in range(1, count)]


def joined_along(parts, dim):
    parts = jnp.moveaxis(parts, 0, dim)
    shape = parts.shape
    return parts.reshape(*shape[:dim], shape[dim] * shape[dim + 1], *shape[dim + 2 :])


def several_exchanges(x, axis, pieces, split_dim, concat_dim):
    parts = split_up(x, split_dim, lax.axis_size(axis))
    split_at = max(range(1, max(2, parts.ndim - 1)), key=lambda d: parts.shape[d])
    gathered = []
    for section in jnp.split(parts, edges_of(parts.shape[split_at], pieces), axis=split_at):
        if section.size:
            gathered.append(lax.all_to_all(section, axis, split_axis=0, concat_axis=0, tiled=True))
    return joined_along(jnp.concatenate(gathered, axis=split_at), concat_dim)


def mode_table(count):
    rank = jnp.arange(count)
    angle = 2.0 * jnp.pi / count * (rank[:, None] * rank[None, :] % count).astype(jnp.float32)
    return (jnp.cos(angle) + jnp.sin(angle)) * count ** (-0.5)


def transform_dim(values, dim):
    moved = jnp.tensordot(
        values, mode_table(values.shape[dim]), axes=([dim], [0]), precision=lax.Precision.HIGHEST
    )
    return jnp.moveaxis(moved, -1, dim)


def per_device(density, symbol_x, symbol_y, symbol_z):
    part_values = density
    part_values = transform_dim(part_values, 0)
    part_values = lax.all_to_all(part_values, "left", split_axis=0, concat_axis=1, tiled=True)
    part_values = transform_dim(part_values, 1)
    block_values = part_values
    block_values = several_exchanges(block_values, "right", 2, 1, 2)
    block_values = transform_dim(block_values, 2)
    share_x = block_values.shape[0]
    part_x = lax.dynamic_slice_in_dim(symbol_x, lax.axis_index("left") * share_x, share_x)
    share_y = block_values.shape[1]
    part_y = lax.dynamic_slice_in_dim(symbol_y, lax.axis_index("right") * share_y, share_y)
    symbol = part_x[:, None, None] + part_y[None, :, None] + symbol_z[None, None, :]
    block_values = block_values * lax.rsqrt(symbol)
    return block_values


def solution(mesh):
    return jax.shard_map(
        per_device,
        mesh=mesh,
        in_specs=(P(None, "left", "right"), P(), P(), P()),
        out_specs=P("left", "right", None),
        check_vma=False,
    )
```

profile of v0, /device:TPU:1, one launch (start us, length us, event | category | flops | bytes accessed | tf_op | source)
XLA Modules:
  0.0 664.2 jit_solution(314109085938783773)
XLA Ops:
  0.0 4.2 fusion.57
  4.2 38.2 %fusion.5 = f32[512,16,512]{2,0,1:T(8,128)S(1)} fusion(f32[512,16,512]{2,1,0:T(8,128)} %param.4, f32[512,512,1]{0,1,2:T(8,128)S(1)} %fusion.57), kind=kOutput, calls=%fused_computation.10 | convolution fusion | flops 25769803776 | bytes 34603008 | tf_op jit(solution)/shard_map/dot_general | solution.py:43
  42.4 17.2 %copy.9 = f32[512,16,512]{2,1,0:T(8,128)S(1)} copy(f32[512,16,512]{2,0,1:T(8,128)S(1)} %fusion.5) | data formatting | bytes 33554432 | tf_op jit(solution)/shard_map/dot_general | solution.py:43
  59.6 193.5 %all_to_all.28 = f32[512,16,512]{2,1,0:T(8,128)S(1)} all-to-all(f32[512,16,512]{2,1,0:T(8,128)S(1)} %copy.9), channel_id=1, replica_groups=mesh['left'=32,'right'=4] {'left'}, dimensions={0} | all-to-all | bytes 33554432 | tf_op jit(solution)/shard_map/all_to_all | solution.py:52
  253.1 6.4 copy.10
  259.5 56.4 %fusion.27 = f32[16,512,512]{1,2,0:T(8,128)} fusion(f32[16,512,512]{2,1,0:T(8,128)} %bitcast.37), kind=kOutput, calls=%fused_computation.31 | convolution fusion | flops 25773998080 | bytes 33554432 | tf_op jit(solution)/shard_map/dot_general | solution.py:43
  316.0 6.9 %copy.18 = f32[16,4,128,512]{3,2,0,1:T(8,128)S(1)} copy(f32[16,4,128,512]{3,2,1,0:T(8,128)} %bitcast.38) | data formatting | bytes 33554432 | tf_op jit(solution)/shard_map/reshape | solution.py:9
  322.9 6.9 %fusion.48 = (f32[4,16,64,512]{3,2,1,0:T(8,128)}, f32[4,16,64,512]{3,2,1,0:T(8,128)}) fusion(f32[4,16,128,512]{3,2,1,0:T(8,128)S(1)} %bitcast.35), kind=kLoop, calls=%fused_computation.54 | loop fusion | bytes 33554432 | tf_op jit(solution)/shard_map/split | solution.py:30
  329.8 103.2 %all_to_all.29 = f32[4,16,64,512]{3,2,1,0:T(8,128)} all-to-all(f32[4,16,64,512]{3,2,1,0:T(8,128)} %get-tuple-element.5), channel_id=1, replica_groups=mesh['left'=32,'right'=4] {'right'}, dimensions={0} | all-to-all | bytes 16777216 | tf_op jit(solution)/shard_map/all_to_all | solution.py:32
  433.1 6.6 all-to-all-start.2
  439.7 0.8 dynamic_slice.7
  440.4 0.8 dynamic_slice.6
  441.2 0.1 broadcast_add_fusion
  441.3 67.7 %fusion.59 = f32[2048,2048,1]{1,0,2:T(8,128)} fusion(), kind=kLoop, calls=%fused_computation.8.clone.clone.clone.1 | loop fusion | flops 67108864 | bytes 16777216 | tf_op jit(solution)/shard_map/dot_general | solution.py:43
  509.0 24.5 %all-to-all-done.2 = f32[4,16,64,512]{3,2,1,0:T(8,128)} async-done(((f32[4,16,64,512]{3,2,1,0:T(8,128)}), f32[4,16,64,512]{3,2,1,0:T(8,128)}, u32[]{:S(2)}, u32[]{:S(2)}) %all-to-all-start.2) | async-done | bytes 8388640 | tf_op jit(solution)/shard_map/all_to_all | solution.py:32
  533.4 6.9 %maximum_bitcast_fusion = f32[4,16,16,8,512]{4,3,2,1,0:T(8,128)S(1)} fusion(f32[4,16,64,512]{3,2,1,0:T(8,128)} %all-to-all-done.2, f32[4,16,64,512]{3,2,1,0:T(8,128)} %all_to_all.29), kind=kLoop, calls=%fused_computation.6 | loop fusion | flops 4194304 | bytes 33554432
  540.3 0.0 copy-start
  540.4 6.2 copy.13
  546.6 0.0 copy-done
  546.6 117.4 %rsqrt_multiply_fusion = f32[16,128,2048]{2,1,0:T(8,128)} fusion(f32[2048]{0:T(1024)S(1)} %copy-done, f32[16,128]{1,0:T(8,128)S(1)} %broadcast_add_fusion, f32[16,128,2048]{2,1,0:T(8,128)} %bitcast.39, f32[2048,2048,1]{1,0,2:T(8,128)} %fusion.59), kind=kOutput, calls=%fused_computation.12 | convolution fusion | flops 103087603712 | bytes 50348032 | tf_op jit(solution)/shard_map/dot_general | solution.py:43
Async XLA Ops:
  433.1 100.4 %all-to-all-start.2 = ((f32[4,16,64,512]{3,2,1,0:T(8,128)}), f32[4,16,64,512]{3,2,1,0:T(8,128)}, u32[]{:S(2)}, u32[]{:S(2)}) async-start(f32[4,16,64,512]{3,2,1,0:T(8,128)} %get-tuple-element.6), calls=%async_computation.2 | async-start | bytes 16777216 | tf_op jit(solution)/shard_map/all_to_all | solution.py:32
  540.3 6.2 copy-start
where the time goes:
time: 668 us; the launch traced here: 664 us
  blocking collectives  297 us (44%)
  matrix products  212 us (32%)
  other arithmetic  78.8 us (12%)
  local copies, waits for them, and re-layouts  45.2 us (7%)
  waiting for transfers between devices  24.5 us (4%)
    dot_general x3, matrix products, transform_dim(): jnp.tensordot(values, mode_table(values.shape[dim]), axes=([dim], [0]), p...  212 us
    all_to_all x1, blocking collectives, per_device(): lax.all_to_all(part_values, 'left', split_axis=0, concat_axis=1, tiled=True)  194 us
    all_to_all x1, blocking collectives, several_exchanges(): lax.all_to_all(section, axis, split_axis=0, concat_axis=0, tiled=True)  103 us
    dot_general x2, other arithmetic, transform_dim(): jnp.tensordot(values, mode_table(values.shape[dim]), axes=([dim], [0]), p...  71.8 us
    all_to_all x1, waiting for transfers between devices, several_exchanges(): lax.all_to_all(section, axis, split_axis=0, concat_axis=0, tiled=True)  24.5 us
    dot_general x1, local copies, waits for them, and re-layouts, transform_dim(): jnp.tensordot(values, mode_table(values.shape[dim]), axes=([dim], [0]), p...  17.2 us
  transfers between devices with their start and end apart: 1, of which 1 were waited for; matrix products, arithmetic and copies ran while one was open for 10% of the time, Pallas kernels for 0%

commit v1 on v0

v1 whole, which is shorter than its diff:
```python
import functools

import jax
import jax.numpy as jnp
import numpy as np
from jax import lax
from jax.experimental import pallas as pl
from jax.experimental.pallas import tpu as pltpu
from jax.sharding import PartitionSpec as P

CUTS = (0, 2, 7, 11, 14, 16)
F32 = jnp.float32
BF16 = jnp.bfloat16


def turns(rows, cols, count):
    return 2.0 * np.pi / count * (np.asarray(rows)[:, None] * np.asarray(cols)[None, :] % count)


def mode_rows(rows, cols, count):
    angle = turns(rows, cols, count)
    return ((np.cos(angle) + np.sin(angle)) * count**-0.5).astype(np.float32)


def np_halves(table):
    high = table.astype(jnp.bfloat16)
    low = (table - high.astype(np.float32)).astype(jnp.bfloat16)
    return jnp.asarray(high), jnp.asarray(low)


def halves(value):
    high = value.astype(BF16)
    return high, (value - high.astype(F32)).astype(BF16)


def dot(a, b):
    return jnp.dot(a, b, preferred_element_type=F32)


def x_kernel(values, even_high, even_low, odd_high, odd_low, out):
    count, rows, lanes = values.shape
    half = count // 2
    flat = values.reshape(count * rows, lanes)
    flat_out = out.reshape(count * rows, lanes)
    for row in range(0, rows, 2):
        first = [flat[pl.ds(row + k, half, stride=rows), :] for k in range(2)]
        second = [flat[pl.ds(half * rows + row + k, half, stride=rows), :] for k in range(2)]
        first = jnp.concatenate(first, axis=1)
        second = jnp.concatenate(second, axis=1)
        for parity, mixed, high, low in (
            (0, first + second, even_high, even_low),
            (1, first - second, odd_high, odd_low),
        ):
            mixed_high, mixed_low = halves(mixed)
            done = dot(high[...], mixed_high) + dot(low[...], mixed_high) + dot(high[...], mixed_low)
            for k in range(2):
                flat_out[pl.ds(parity * rows + row + k, half, stride=2 * rows), :] = done[:, k * lanes : (k + 1) * lanes]


def fold_tables(count):
    first = np.arange(count // 2)
    even = mode_rows(np.arange(0, count, 2), first, count)
    odd = mode_rows(np.arange(1, count, 2), first, count)
    return np_halves(even) + np_halves(odd)


def x_modes(density):
    nx, ny, nz = density.shape
    half = nx // 2
    rows, lanes = 8, 128
    block = pl.BlockSpec((nx, rows, lanes), lambda i, k: (0, i, k))
    fixed = pl.BlockSpec((half, half), lambda i, k: (0, 0))
    return pl.pallas_call(
        x_kernel,
        grid=(ny // rows, nz // lanes),
        in_specs=[block] + [fixed] * 4,
        out_specs=block,
        out_shape=jax.ShapeDtypeStruct((nx, ny, nz), F32),
        name="x_modes",
    )(density, *fold_tables(nx))


def y_kernel(own, values, *rest, right):
    tables, outs = rest[: 2 * right], rest[2 * right :]
    parts, _, part, nz = values.shape
    share = outs[0].shape[1]
    high = jnp.concatenate([table[...] for table in tables[:right]], axis=0)
    low = jnp.concatenate([table[...] for table in tables[right:]], axis=0)
    full_high, full_low = halves(values[...].reshape(parts * part, nz))
    done = dot(high, full_high) + dot(low, full_high) + dot(high, full_low)
    for k, out in enumerate(outs):
        out[0] = done[k * share : (k + 1) * share]


def y_modes(values, own, lo, hi, right):
    parts, _, part, nz = values.shape
    ny = parts * part
    share = ny // right
    tables = np_halves(mode_rows(np.arange(ny), np.arange(ny), ny))
    pick = [pl.BlockSpec((share, ny), lambda j, own, k=k: (own[0] ^ k, 0)) for k in range(right)]
    return pl.pallas_call(
        functools.partial(y_kernel, right=right),
        grid_spec=pltpu.PrefetchScalarGridSpec(
            num_scalar_prefetch=1,
            grid=(hi - lo,),
            in_specs=[pl.BlockSpec((parts, 1, part, nz), lambda j, own: (0, lo + j, 0, 0))] + pick * 2,
            out_specs=[pl.BlockSpec((1, share, nz), lambda j, own: (j, 0, 0))] * right,
        ),
        out_shape=[jax.ShapeDtypeStruct((hi - lo, share, nz), F32)] * right,
        name="y_modes",
    )(own, values, *[table for table in tables for _ in range(right)])


def z_kernel(part_x, high, low, part_y, symbol_z, *rest, lo, count, summed, last):
    values = rest[:count]
    out, mine = rest[-2:]
    own, share, width = values[0].shape
    rows = own * share

    @pl.when(pl.program_id(0) == 0)
    def _():
        for r in range(count):
            value_high, value_low = halves(values[r][...].reshape(rows, width))
            mine[:rows, r * width : (r + 1) * width] = value_high
            mine[rows:, r * width : (r + 1) * width] = value_low

    both = dot(mine[...], high[...])
    done = both[:rows] + both[rows:] + dot(mine[:rows], low[...])
    for j in range(own):
        result = done[j * share : (j + 1) * share]
        if summed:
            result = result + rest[count][j]
        if last:
            result = result * lax.rsqrt(part_x[lo + j] + part_y[...] + symbol_z[...])
        out[j] = result


def z_modes(values, places, tables, symbols, lo, sums=None, out=None, last=True):
    count = len(values)
    own, share, width = values[0].shape
    part_x, part_y, symbol_z = symbols
    nz = symbol_z.shape[1]
    lanes = 256
    cols = pl.BlockSpec((count * width, lanes), lambda n: (places[0] // count, n))
    sum_block = pl.BlockSpec((own, share, lanes), lambda n: (0, 0, n))
    in_specs = [
        pl.BlockSpec(memory_space=pltpu.SMEM),
        cols,
        cols,
        pl.BlockSpec((share, 1), lambda n: (0, 0)),
        pl.BlockSpec((1, lanes), lambda n: (0, n)),
    ] + [pl.BlockSpec((own, share, width), lambda n: (0, 0, 0))] * count
    args = [part_x, *tables, part_y, symbol_z, *values]
    if sums is not None:
        in_specs.append(sum_block)
        args.append(sums)
    aliases = {}
    if out is not None:
        aliases = {len(args): 0}
        in_specs.append(pl.BlockSpec(memory_space=pl.ANY))
        args.append(out)
    full_block = pl.BlockSpec((pl.Element(own), pl.Element(share), pl.Element(lanes)), lambda n: (lo, 0, n * lanes))
    return pl.pallas_call(
        functools.partial(z_kernel, lo=lo, count=count, summed=sums is not None, last=last),
        grid=(nz // lanes,),
        in_specs=in_specs,
        out_specs=full_block if last else sum_block,
        out_shape=jax.ShapeDtypeStruct((part_x.shape[0] if last else own, share, nz), F32),
        scratch_shapes=[pltpu.VMEM((2 * own * share, count * width), BF16)],
        input_output_aliases=aliases,
        name="z_modes",
    )(*args)


def run_halves(table):
    high = lax.reduce_precision(table, 8, 7)
    return high.astype(BF16), (table - high).astype(BF16)


def angles(rows, cols, count):
    return 2.0 * jnp.pi / count * (rows[:, None] * cols[None, :] % count).astype(F32)


def z_tables(nz, right, own, zero):
    step = 64
    share = nz // right
    cols = jnp.arange(nz) + zero
    rank = jnp.arange(0, nz, step) + zero
    coarse = angles(((rank // share) ^ own) * share + rank % share, cols, nz)
    fine = angles(jnp.arange(step), cols, nz)
    cos, sin = jnp.cos(fine) * nz**-0.5, jnp.sin(fine) * nz**-0.5
    near, back, cos, sin = lax.optimization_barrier((cos + sin, cos - sin, jnp.cos(coarse), jnp.sin(coarse)))
    high, low = run_halves(cos[:, None, :] * near[None] + sin[:, None, :] * back[None])
    return high.reshape(nz, nz), low.reshape(nz, nz)


def per_device(density, symbol_x, symbol_y, symbol_z):
    left = lax.axis_size("left")
    right = lax.axis_size("right")
    nx, ny_part, nz_part = density.shape
    share_x = nx // left
    share_y = ny_part * left // right
    a = x_modes(density).reshape(left, share_x, ny_part, nz_part)
    at_left = lax.axis_index("left").astype(jnp.int32)
    at_right = lax.axis_index("right").astype(jnp.int32)[None]
    a, at_left, at_right = lax.optimization_barrier((a, at_left, at_right))
    a = lax.all_to_all(a, "left", split_axis=0, concat_axis=0, tiled=True)
    sent = []
    for c, (lo, hi) in enumerate(zip(CUTS, CUTS[1:])):
        b = y_modes(a, at_right, lo, hi, right)
        a, mine, at_left, zero = lax.optimization_barrier((a, b[0], at_left, jnp.int32(0)))
        met = [mine]
        for k in range(1, right):
            met.append(lax.ppermute(b[k], "right", [(r, r ^ k) for r in range(right)]))
        sent.append(met)
        if c == 1:
            at = at_right[0] + zero
            tables = z_tables(nz_part * right, right, at, zero)
            part_x = lax.dynamic_slice_in_dim(symbol_x, at_left * share_x, share_x)
            part_y = lax.dynamic_slice_in_dim(symbol_y, at * share_y, share_y)[:, None]
            symbols = (part_x, part_y, symbol_z[None])
    out = None
    for c, (lo, hi) in enumerate(zip(CUTS, CUTS[1:])):
        met = sent[c]
        if hi < share_x:
            out = z_modes(met, range(right), tables, symbols, lo, out=out)
        else:
            half = right // 2
            sums = z_modes(met[:half], range(half), tables, symbols, lo, last=False)
            out = z_modes(met[half:], range(half, right), tables, symbols, lo, sums=sums, out=out)
    return out


def solution(mesh):
    return jax.shard_map(
        per_device,
        mesh=mesh,
        in_specs=(P(None, "left", "right"), P(), P(), P()),
        out_specs=P("left", "right", None),
        check_vma=False,
    )
```

time: 668 us -> 479 us (0.72)
  matrix products: 212 us -> 0 us
  Pallas kernels: 0 us -> 142 us
  blocking collectives: 297 us -> 194 us
  waiting for transfers between devices: 24.5 us -> 88.7 us
  other arithmetic: 78.8 us -> 24.3 us
  local copies, waits for them, and re-layouts: 45.2 us -> 4.68 us
  starting transfers between devices: 6.63 us -> 23.8 us
    dot_general x3 -> x0, matrix products: 212 us -> none  [transform_dim(): jnp.tensordot(values, mode_table(values.shape[dim]), axes=([dim], [0]), p...]
    pallas_call x0 -> x12, Pallas kernels: none -> 142 us  [the longest x6 92.9 us: z_modes(): pl.pallas_call(functools.partial(z_kernel, lo=lo, count=count, summed=sum...]
    all_to_all x2 -> x1, blocking collectives: 297 us -> 194 us  [per_device(): a = lax.all_to_all(a, 'left', split_axis=0, concat_axis=0, tiled=True)]
    ppermute x0 -> x15, waiting for transfers between devices: none -> 88.7 us  [per_device(): met.append(lax.ppermute(b[k], 'right', [(r, r ^ k) for r in range(right)]))]
    dot_general x2 -> x0, other arithmetic: 71.8 us -> none  [transform_dim(): jnp.tensordot(values, mode_table(values.shape[dim]), axes=([dim], [0]), p...]
    all_to_all x1 -> x0, waiting for transfers between devices: 24.5 us -> none  [several_exchanges(): lax.all_to_all(section, axis, split_axis=0, concat_axis=0, tiled=True)]
    ppermute x0 -> x15, starting transfers between devices: none -> 23.8 us  [per_device(): met.append(lax.ppermute(b[k], 'right', [(r, r ^ k) for r in range(right)]))]
    dot_general x1 -> x0, local copies, waits for them, and re-layouts: 17.2 us -> none  [transform_dim(): jnp.tensordot(values, mode_table(values.shape[dim]), axes=([dim], [0]), p...]
  transfers between devices with their start and end apart: 1 -> 15, of which waited for: 1 -> 3; matrix products, arithmetic and copies ran while one was open for 10% -> 6% of each run, Pallas kernels for 0% -> 19%
where the time goes in v1:
time: 479 us; the launch traced here: 477 us
  blocking collectives  194 us (41%)
  Pallas kernels  142 us (30%)
  waiting for transfers between devices  88.7 us (19%)
  other arithmetic  24.3 us (5%)
  starting transfers between devices  23.8 us (5%)
    all_to_all x1, blocking collectives, per_device(): a = lax.all_to_all(a, 'left', split_axis=0, concat_axis=0, tiled=True)  194 us
    pallas_call x6, Pallas kernels, z_modes(): pl.pallas_call(functools.partial(z_kernel, lo=lo, count=count, summed=sum...  92.9 us
    ppermute x15, waiting for transfers between devices, per_device(): met.append(lax.ppermute(b[k], 'right', [(r, r ^ k) for r in range(right)]))  88.7 us
    pallas_call x5, Pallas kernels, y_modes(): pl.pallas_call(functools.partial(y_kernel, right=right), grid_spec=pltpu....  30.4 us
    ppermute x15, starting transfers between devices, per_device(): met.append(lax.ppermute(b[k], 'right', [(r, r ^ k) for r in range(right)]))  23.8 us
    pallas_call x1, Pallas kernels, x_modes(): pl.pallas_call(x_kernel, grid=(ny // rows, nz // lanes), in_specs=[block]...  18.4 us
    convert_element_type x1, other arithmetic, run_halves(): return (high.astype(BF16), (table - high).astype(BF16))  12.4 us
  transfers between devices with their start and end apart: 15, of which 3 were waited for; matrix products, arithmetic and copies ran while one was open for 6% of the time, Pallas kernels for 19%

profile of v1, /device:TPU:1, one launch (start us, length us, event | category | flops | bytes accessed | tf_op | source)
XLA Modules:
  0.0 477.1 jit_solution(5983174978434172778)
XLA Ops:
  0.0 18.4 %x_modes.1 = f32[512,16,512]{2,1,0:T(8,128)} custom-call(f32[512,16,512]{2,1,0:T(8,128)} %values.1, bf16[256,256]{1,0:T(8,128)(2,1)} %constant.84.clone.even_high, bf16[256,256]{1,0:T(8,128)(2,1)} %constant.85.clone.even_low, bf16[256,256]{1,0:T(8,128)(2,1)} %constant.86.clone.odd_high, bf16[256,256]{1,0:T(8,128)(2,1)} %constant.87.clone.odd_low), custom_call_target="tpu_custom_call" | custom-call | tf_op jit(solution)/shard_map/x_modes/pallas_call | solution.py:73
  18.4 193.8 %all_to_all.5.values = f32[32,16,16,512]{3,2,1,0:T(8,128)} all-to-all(f32[32,16,16,512]{3,2,1,0:T(8,128)} %bitcast.9), channel_id=1, replica_groups=mesh['left'=32,'right'=4] {'left'}, dimensions={0} | all-to-all | bytes 33554432 | tf_op jit(solution)/shard_map/all_to_all | solution.py:207
  212.2 4.5 y_modes.5
  216.7 8.6 %y_modes.6 = (f32[5,128,512]{2,1,0:T(8,128)}, f32[5,128,512]{2,1,0:T(8,128)}, f32[5,128,512]{2,1,0:T(8,128)}, f32[5,128,512]{2,1,0:T(8,128)}) custom-call(s32[1]{0:T(128)} %bitcast.1.own, f32[32,16,16,512]{3,2,1,0:T(8,128)} %all_to_all.5.values, bf16[512,512]{1,0:T(8,128)(2,1)} %constant.88.clone.rest_0_.rest_1_.rest_2_.rest_3_, ...), custom_call_target="tpu_custom_call" | custom-call | tf_op jit(solution)/shard_map/y_modes/pallas_call | solution.py:101
  225.3 7.0 %y_modes.7 = (f32[4,128,512]{2,1,0:T(8,128)}, f32[4,128,512]{2,1,0:T(8,128)}, f32[4,128,512]{2,1,0:T(8,128)}, f32[4,128,512]{2,1,0:T(8,128)}) custom-call(s32[1]{0:T(128)} %bitcast.1.own, f32[32,16,16,512]{3,2,1,0:T(8,128)} %all_to_all.5.values, bf16[512,512]{1,0:T(8,128)(2,1)} %constant.88.clone.rest_0_.rest_1_.rest_2_.rest_3_, ...), custom_call_target="tpu_custom_call" | custom-call | tf_op jit(solution)/shard_map/y_modes/pallas_call | solution.py:101
  232.3 2.2 collective-permute-start.6
  234.5 0.1 collective-permute-start.12
  234.6 2.6 collective-permute-start.13
  237.2 0.9 collective-permute-start.14
  238.2 5.9 %y_modes.8 = (f32[3,128,512]{2,1,0:T(8,128)}, f32[3,128,512]{2,1,0:T(8,128)}, f32[3,128,512]{2,1,0:T(8,128)}, f32[3,128,512]{2,1,0:T(8,128)}) custom-call(s32[1]{0:T(128)} %bitcast.1.own, f32[32,16,16,512]{3,2,1,0:T(8,128)} %all_to_all.5.values, bf16[512,512]{1,0:T(8,128)(2,1)} %constant.88.clone.rest_0_.rest_1_.rest_2_.rest_3_, ...), custom_call_target="tpu_custom_call" | custom-call | tf_op jit(solution)/shard_map/y_modes/pallas_call | solution.py:101
  244.0 4.5 y_modes.9
  248.5 0.0 collective-permute-start.2
  248.5 2.1 fusion.7
  250.6 0.0 collective-permute-done.12.rest_1_
  250.7 0.8 copy-done.7
  251.5 0.5 collective-permute-start.9
  251.9 0.0 collective-permute-done.13.rest_2_
  252.0 0.8 copy-done.8
  252.8 2.6 collective-permute-start.10
  255.4 6.5 %collective-permute-done.14.rest_3_ = f32[2,128,512]{2,1,0:T(8,128)S(1)} collective-permute-done((f32[2,128,512]{2,1,0:T(8,128)}, f32[2,128,512]{2,1,0:T(8,128)S(1)}, u32[]{:S(2)}, u32[]{:S(2)}) %collective-permute-start.14) | collective-permute-done | bytes 524320 | tf_op jit(solution)/shard_map/ppermute | solution.py:214
  261.9 1.4 collective-permute-start.11
  263.3 0.0 collective-permute-done.2.rest_1_
  263.3 1.3 collective-permute-start.7
  264.6 0.0 collective-permute-done.6.rest_1_
  264.6 3.4 collective-permute-start.8
  268.0 1.1 fusion.12
  269.1 8.7 %multiply_add_fusion = f32[32,64,2048]{2,1,0:T(8,128)} fusion(f32[64,2048]{1,0:T(8,128)S(1)} %get-tuple-element.56, f32[32,2048]{1,0:T(8,128)S(1)} %get-tuple-element.55, f32[64,2048]{1,0:T(8,128)S(1)} %get-tuple-element.54, f32[32,2048]{1,0:T(8,128)S(1)} %get-tuple-element.53), kind=kLoop, calls=%fused_computation.3 | loop fusion | flops 12582912 | bytes 18350080 | tf_op jit(solution)/shard_map/add | solution.py:193
  277.8 61.3 %collective-permute-done.7.rest_2_ = f32[4,128,512]{2,1,0:T(8,128)S(1)} collective-permute-done((f32[4,128,512]{2,1,0:T(8,128)}, f32[4,128,512]{2,1,0:T(8,128)S(1)}, u32[]{:S(2)}, u32[]{:S(2)}) %collective-permute-start.7) | collective-permute-done | bytes 1048608 | tf_op jit(solution)/shard_map/ppermute | solution.py:214
  339.1 2.1 collective-permute-start.3
  341.2 20.9 %collective-permute-done.8.rest_3_ = f32[4,128,512]{2,1,0:T(8,128)S(1)} collective-permute-done((f32[4,128,512]{2,1,0:T(8,128)}, f32[4,128,512]{2,1,0:T(8,128)S(1)}, u32[]{:S(2)}, u32[]{:S(2)}) %collective-permute-start.8) | collective-permute-done | bytes 1048608 | tf_op jit(solution)/shard_map/ppermute | solution.py:214
  362.1 2.6 collective-permute-start.4
  364.7 0.0 collective-permute-done.9.rest_1_
  364.7 0.3 collective-permute-start.5
  365.1 2.7 collective-permute-start
  367.8 0.0 collective-permute-done.11.rest_3_
  367.8 0.9 collective-permute-start.1
  368.7 12.4 %fusion = (bf16[2048,2048]{1,0:T(8,128)(2,1)}, bf16[2048,2048]{1,0:T(8,128)(2,1)}) fusion(f32[32,64,2048]{2,1,0:T(8,128)} %multiply_add_fusion), kind=kLoop, calls=%fused_computation.2 | loop fusion | flops 16777216 | bytes 33554432 | tf_op jit(solution)/shard_map/convert_element_type | solution.py:177
  381.1 0.1 dynamic-slice_bitcast_fusion
  381.2 0.7 copy.28.part_y
  381.9 1.3 dynamic_slice.6.part_x
  383.3 9.8 %z_modes.6.rest_2_ = f32[2,128,2048]{2,1,0:T(8,128)} custom-call(f32[16]{0:T(128)} %dynamic_slice.6.part_x, bf16[2048,2048]{1,0:T(8,128)(2,1)} %get-tuple-element.84.high, bf16[2048,2048]{1,0:T(8,128)(2,1)} %get-tuple-element.83.low, f32[128,1]{1,0:T(8,128)} %copy.28.part_y, f32[1,2048]{1,0:T(1,128)} %bitcast.10, f32[2,128,512]{2,1,0:T(8,128)} %get-tuple-element.65.rest_0_, ...), custom_call_target="tpu_custom_call" | custom-call | tf_op jit(solution)/shard_map/z_modes/pallas_call | solution.py:163
  393.1 14.0 %z_modes.7.rest_4_ = f32[16,128,2048]{2,1,0:T(8,128)} custom-call(f32[16]{0:T(128)} %dynamic_slice.6.part_x, bf16[2048,2048]{1,0:T(8,128)(2,1)} %get-tuple-element.84.high, bf16[2048,2048]{1,0:T(8,128)(2,1)} %get-tuple-element.83.low, f32[128,1]{1,0:T(8,128)} %copy.28.part_y, f32[1,2048]{1,0:T(1,128)} %bitcast.11, f32[2,128,512]{2,1,0:T(8,128)} %get-tuple-element.79.rest_0_, ...), custom_call_target="tpu_custom_call" | custom-call | tf_op jit(solution)/shard_map/z_modes/pallas_call | solution.py:163
  407.1 23.1 %z_modes.8.rest_4_ = f32[16,128,2048]{2,1,0:T(8,128)} custom-call(f32[16]{0:T(128)} %dynamic_slice.6.part_x, bf16[2048,2048]{1,0:T(8,128)(2,1)} %get-tuple-element.84.high, bf16[2048,2048]{1,0:T(8,128)(2,1)} %get-tuple-element.83.low, f32[128,1]{1,0:T(8,128)} %copy.28.part_y, f32[1,2048]{1,0:T(1,128)} %bitcast.12, ...), custom_call_target="tpu_custom_call", output_to_operand_aliasing={{}: (9, {})} | custom-call | tf_op jit(solution)/shard_map/z_modes/pallas_call | solution.py:163
  430.2 19.3 %z_modes.9.rest_4_ = f32[16,128,2048]{2,1,0:T(8,128)} custom-call(f32[16]{0:T(128)} %dynamic_slice.6.part_x, bf16[2048,2048]{1,0:T(8,128)(2,1)} %get-tuple-element.84.high, bf16[2048,2048]{1,0:T(8,128)(2,1)} %get-tuple-element.83.low, f32[128,1]{1,0:T(8,128)} %copy.28.part_y, f32[1,2048]{1,0:T(1,128)} %bitcast.13, ...), custom_call_target="tpu_custom_call", output_to_operand_aliasing={{}: (9, {})} | custom-call | tf_op jit(solution)/shard_map/z_modes/pallas_call | solution.py:163
  449.5 0.0 collective-permute-done.5.rest_3_
  449.5 0.9 copy-done.6
  450.4 16.4 %z_modes.10.rest_3_ = f32[16,128,2048]{2,1,0:T(8,128)} custom-call(f32[16]{0:T(128)} %dynamic_slice.6.part_x, bf16[2048,2048]{1,0:T(8,128)(2,1)} %get-tuple-element.84.high, bf16[2048,2048]{1,0:T(8,128)(2,1)} %get-tuple-element.83.low, f32[128,1]{1,0:T(8,128)} %copy.28.part_y, f32[1,2048]{1,0:T(1,128)} %bitcast.14, ...), custom_call_target="tpu_custom_call", output_to_operand_aliasing={{}: (9, {})} | custom-call | tf_op jit(solution)/shard_map/z_modes/pallas_call | solution.py:163
  466.9 10.2 %z_modes.11 = f32[16,128,2048]{2,1,0:T(8,128)} custom-call(f32[16]{0:T(128)} %dynamic_slice.6.part_x, bf16[2048,2048]{1,0:T(8,128)(2,1)} %get-tuple-element.84.high, bf16[2048,2048]{1,0:T(8,128)(2,1)} %get-tuple-element.83.low, f32[128,1]{1,0:T(8,128)} %copy.28.part_y, f32[1,2048]{1,0:T(1,128)} %bitcast.15, ...), custom_call_target="tpu_custom_call", output_to_operand_aliasing={{}: (8, {})} | custom-call | tf_op jit(solution)/shard_map/z_modes/pallas_call | solution.py:163
  (28 shorter events, 0.1 us)
Async XLA Ops:
  0.0 381.1 %copy-start = (f32[512]{0:T(512)S(1)}, f32[512]{0:T(512)}, u32[]{:S(2)}) copy-start(f32[512]{0:T(512)} %param.20) | copy-start | bytes 6148
  216.7 17.8 %copy-start.11 = (f32[2,128,512]{2,1,0:T(8,128)S(1)}, f32[2,128,512]{2,1,0:T(8,128)}, u32[]{:S(2)}) copy-start(f32[2,128,512]{2,1,0:T(8,128)} %get-tuple-element.80) | copy-start | bytes 1572868
  216.7 17.9 %copy-start.10 = (f32[2,128,512]{2,1,0:T(8,128)S(1)}, f32[2,128,512]{2,1,0:T(8,128)}, u32[]{:S(2)}) copy-start(f32[2,128,512]{2,1,0:T(8,128)} %get-tuple-element.81) | copy-start | bytes 1572868
  232.3 32.3 %collective-permute-start.6 = (f32[4,128,512]{2,1,0:T(8,128)}, f32[4,128,512]{2,1,0:T(8,128)}, u32[]{:S(2)}, u32[]{:S(2)}) collective-permute-start(f32[4,128,512]{2,1,0:T(8,128)} %get-tuple-element.72), channel_id=1, source_target_pairs={{0,1},{1,0},{2,3},{3,2},{4,5},{5,4},{6,7},{7,6},{8,9},{9,8},{10,11... | collective-permute-start | bytes 3145736 | tf_op jit(solution)/shard_map/ppermute | solution.py:214
  234.5 16.1 %collective-permute-start.12 = (f32[2,128,512]{2,1,0:T(8,128)S(1)}, f32[2,128,512]{2,1,0:T(8,128)S(1)}, u32[]{:S(2)}, u32[]{:S(2)}) collective-permute-start(f32[2,128,512]{2,1,0:T(8,128)S(1)} %copy-done.11), channel_id=1, source_target_pairs={{0,1},{1,0},{2,3},{3,2},{4,5},{5,4},{6,7},{7,6},{8,9},{9,8},{10,11... | collective-permute-start | bytes 1572872 | tf_op jit(solution)/shard_map/ppermute | solution.py:214
  234.6 17.3 %collective-permute-start.13 = (f32[2,128,512]{2,1,0:T(8,128)S(1)}, f32[2,128,512]{2,1,0:T(8,128)S(1)}, u32[]{:S(2)}, u32[]{:S(2)}) collective-permute-start(f32[2,128,512]{2,1,0:T(8,128)S(1)} %copy-done.10), channel_id=1, source_target_pairs={{0,2},{1,3},{2,0},{3,1},{4,6},{5,7},{6,4},{7,5},{8,10},{9,11},{10,... | collective-permute-start | bytes 1572872 | tf_op jit(solution)/shard_map/ppermute | solution.py:214
  237.2 24.6 %collective-permute-start.14 = (f32[2,128,512]{2,1,0:T(8,128)}, f32[2,128,512]{2,1,0:T(8,128)S(1)}, u32[]{:S(2)}, u32[]{:S(2)}) collective-permute-start(f32[2,128,512]{2,1,0:T(8,128)} %get-tuple-element.82), channel_id=1, source_target_pairs={{0,3},{1,2},{2,1},{3,0},{4,7},{5,6},{6,5},{7,4},{8,11},{9,10},{10,... | collective-permute-start | bytes 1572872 | tf_op jit(solution)/shard_map/ppermute | solution.py:214
  248.5 14.8 %collective-permute-start.2 = (f32[2,128,512]{2,1,0:T(8,128)}, f32[2,128,512]{2,1,0:T(8,128)}, u32[]{:S(2)}, u32[]{:S(2)}) collective-permute-start(f32[2,128,512]{2,1,0:T(8,128)} %get-tuple-element.66), channel_id=1, source_target_pairs={{0,1},{1,0},{2,3},{3,2},{4,5},{5,4},{6,7},{7,6},{8,9},{9,8},{10,11... | collective-permute-start | bytes 1572872 | tf_op jit(solution)/shard_map/ppermute | solution.py:214
  250.6 0.8 copy-start.7
  251.5 113.3 %collective-permute-start.9 = (f32[5,128,512]{2,1,0:T(8,128)}, f32[5,128,512]{2,1,0:T(8,128)S(1)}, u32[]{:S(2)}, u32[]{:S(2)}) collective-permute-start(f32[5,128,512]{2,1,0:T(8,128)} %get-tuple-element.76), channel_id=1, source_target_pairs={{0,1},{1,0},{2,3},{3,2},{4,5},{5,4},{6,7},{7,6},{8,9},{9,8},{10,11... | collective-permute-start | bytes 3932168 | tf_op jit(solution)/shard_map/ppermute | solution.py:214
  252.0 0.8 copy-start.8
  252.8 112.3 %collective-permute-start.10 = (f32[5,128,512]{2,1,0:T(8,128)}, f32[5,128,512]{2,1,0:T(8,128)S(1)}, u32[]{:S(2)}, u32[]{:S(2)}) collective-permute-start(f32[5,128,512]{2,1,0:T(8,128)} %get-tuple-element.77), channel_id=1, source_target_pairs={{0,2},{1,3},{2,0},{3,1},{4,6},{5,7},{6,4},{7,5},{8,10},{9,11},{10,... | collective-permute-start | bytes 3932168 | tf_op jit(solution)/shard_map/ppermute | solution.py:214
  261.9 77.2 %copy-start.9 = (f32[2,128,512]{2,1,0:T(8,128)}, f32[2,128,512]{2,1,0:T(8,128)S(1)}, u32[]{:S(2)}) copy-start(f32[2,128,512]{2,1,0:T(8,128)S(1)} %collective-permute-done.14.rest_3_) | copy-start | bytes 1572868
  261.9 105.9 %collective-permute-start.11 = (f32[5,128,512]{2,1,0:T(8,128)}, f32[5,128,512]{2,1,0:T(8,128)}, u32[]{:S(2)}, u32[]{:S(2)}) collective-permute-start(f32[5,128,512]{2,1,0:T(8,128)} %get-tuple-element.78), channel_id=1, source_target_pairs={{0,3},{1,2},{2,1},{3,0},{4,7},{5,6},{6,5},{7,4},{8,11},{9,10},{10,... | collective-permute-start | bytes 3932168 | tf_op jit(solution)/shard_map/ppermute | solution.py:214
  263.3 75.7 %collective-permute-start.7 = (f32[4,128,512]{2,1,0:T(8,128)}, f32[4,128,512]{2,1,0:T(8,128)S(1)}, u32[]{:S(2)}, u32[]{:S(2)}) collective-permute-start(f32[4,128,512]{2,1,0:T(8,128)} %get-tuple-element.73), channel_id=1, source_target_pairs={{0,2},{1,3},{2,0},{3,1},{4,6},{5,7},{6,4},{7,5},{8,10},{9,11},{10,... | collective-permute-start | bytes 3145736 | tf_op jit(solution)/shard_map/ppermute | solution.py:214
  264.6 97.5 %collective-permute-start.8 = (f32[4,128,512]{2,1,0:T(8,128)}, f32[4,128,512]{2,1,0:T(8,128)S(1)}, u32[]{:S(2)}, u32[]{:S(2)}) collective-permute-start(f32[4,128,512]{2,1,0:T(8,128)} %get-tuple-element.74), channel_id=1, source_target_pairs={{0,3},{1,2},{2,1},{3,0},{4,7},{5,6},{6,5},{7,4},{8,11},{9,10},{10,... | collective-permute-start | bytes 3145736 | tf_op jit(solution)/shard_map/ppermute | solution.py:214
  339.1 26.0 %copy-start.4 = (f32[4,128,512]{2,1,0:T(8,128)}, f32[4,128,512]{2,1,0:T(8,128)S(1)}, u32[]{:S(2)}) copy-start(f32[4,128,512]{2,1,0:T(8,128)S(1)} %collective-permute-done.7.rest_2_) | copy-start | bytes 3145732
  339.1 110.5 %collective-permute-start.3 = (f32[3,128,512]{2,1,0:T(8,128)}, f32[3,128,512]{2,1,0:T(8,128)S(1)}, u32[]{:S(2)}, u32[]{:S(2)}) collective-permute-start(f32[3,128,512]{2,1,0:T(8,128)} %get-tuple-element.68), channel_id=1, source_target_pairs={{0,1},{1,0},{2,3},{3,2},{4,5},{5,4},{6,7},{7,6},{8,9},{9,8},{10,11... | collective-permute-start | bytes 2359304 | tf_op jit(solution)/shard_map/ppermute | solution.py:214
  362.1 3.0 copy-start.5
  362.1 87.4 %collective-permute-start.4 = (f32[3,128,512]{2,1,0:T(8,128)}, f32[3,128,512]{2,1,0:T(8,128)}, u32[]{:S(2)}, u32[]{:S(2)}) collective-permute-start(f32[3,128,512]{2,1,0:T(8,128)} %get-tuple-element.69), channel_id=1, source_target_pairs={{0,2},{1,3},{2,0},{3,1},{4,6},{5,7},{6,4},{7,5},{8,10},{9,11},{10,... | collective-permute-start | bytes 2359304 | tf_op jit(solution)/shard_map/ppermute | solution.py:214
  364.7 16.4 %copy-start.2 = (f32[5,128,512]{2,1,0:T(8,128)}, f32[5,128,512]{2,1,0:T(8,128)S(1)}, u32[]{:S(2)}) copy-start(f32[5,128,512]{2,1,0:T(8,128)S(1)} %collective-permute-done.9.rest_1_) | copy-start | bytes 3932164
  364.7 84.8 %collective-permute-start.5 = (f32[3,128,512]{2,1,0:T(8,128)}, f32[3,128,512]{2,1,0:T(8,128)}, u32[]{:S(2)}, u32[]{:S(2)}) collective-permute-start(f32[3,128,512]{2,1,0:T(8,128)} %get-tuple-element.70), channel_id=1, source_target_pairs={{0,3},{1,2},{2,1},{3,0},{4,7},{5,6},{6,5},{7,4},{8,11},{9,10},{10,... | collective-permute-start | bytes 2359304 | tf_op jit(solution)/shard_map/ppermute | solution.py:214
  365.1 16.0 %copy-start.3 = (f32[5,128,512]{2,1,0:T(8,128)}, f32[5,128,512]{2,1,0:T(8,128)S(1)}, u32[]{:S(2)}) copy-start(f32[5,128,512]{2,1,0:T(8,128)S(1)} %collective-permute-done.10.rest_2_) | copy-start | bytes 3932164
  365.1 101.8 %collective-permute-start = (f32[2,128,512]{2,1,0:T(8,128)}, f32[2,128,512]{2,1,0:T(8,128)}, u32[]{:S(2)}, u32[]{:S(2)}) collective-permute-start(f32[2,128,512]{2,1,0:T(8,128)} %get-tuple-element.62), channel_id=1, source_target_pairs={{0,2},{1,3},{2,0},{3,1},{4,6},{5,7},{6,4},{7,5},{8,10},{9,11},{10,... | collective-permute-start | bytes 1572872 | tf_op jit(solution)/shard_map/ppermute | solution.py:214
  367.8 99.1 %collective-permute-start.1 = (f32[2,128,512]{2,1,0:T(8,128)}, f32[2,128,512]{2,1,0:T(8,128)}, u32[]{:S(2)}, u32[]{:S(2)}) collective-permute-start(f32[2,128,512]{2,1,0:T(8,128)} %get-tuple-element.63), channel_id=1, source_target_pairs={{0,3},{1,2},{2,1},{3,0},{4,7},{5,6},{6,5},{7,4},{8,11},{9,10},{10,... | collective-permute-start | bytes 1572872 | tf_op jit(solution)/shard_map/ppermute | solution.py:214
  449.5 0.9 copy-start.6
  450.4 26.7 %copy-start.1 = (f32[512]{0:T(512)S(1)}, f32[512]{0:T(512)}, u32[]{:S(2)}) copy-start(f32[512]{0:T(512)} %param.20) | copy-start | bytes 6148
